TPU v7x, 512 devices: a whole 4x8x8 slice. The times are simulated.
512 devices in a mesh: section: 4 (over x), ctx: 64 (over y, z), mp: 2 (over core).
Axes of the slice: x: 4, y: 8, z: 8, core: 2. Of those that a mesh axis runs over, the one named last changes fastest.
Arguments:
- head_input: bfloat16 [4, 16384, 2048], P('section', 'ctx', 'mp'), may hold values from -6 to 6
- state_proj: bfloat16 [4, 16384, 256], P('section', 'ctx'), may hold values from -6 to 6
- gate_input: bfloat16 [4, 16384, 2048], P('section', 'ctx', 'mp'), may hold values from -6 to 6
- step_raw: float32 [4, 32, 16384], P('section', 'mp', 'ctx'), may hold values from -2 to 2
- step_bias: float32 [4, 32], P('section', 'mp'), may hold values from -9.5 to -3
- decay_log: float32 [4, 32], P('section', 'mp'), may hold values from -7 to 1.5
- skip_gain: float32 [4, 32], P('section', 'mp'), may hold values from 0.5 to 1.5
- conv_head: float32 [4, 4, 2048], P('section', None, 'mp'), may hold values from -3 to 3
- conv_state: float32 [4, 4, 256], P('section'), may hold values from -3 to 3
- norm_gain: float32 [4, 2048], P('section', 'mp'), may hold values from 0.1 to 1.9
- next_weight: bfloat16 [4, 2048, 4096], P('section', 'ctx', 'mp'), may hold values from -0.125 to 0.125
Outputs:
- projected: bfloat16 [4, 16384, 4096], P('section', 'ctx', 'mp')
All inputs are finite; a program needn't handle non-finite values.
Results may differ from a plain program's by a relative error of at most 0.0087.
Values may be sent and summed in bfloat16 or wider, within the bound.
No kernel may reach another device: no remote copies, remote signals or barrier semaphores. Data moves between devices by JAX's collectives and lax.ppermute only.
A program may use at most 64 MiB of HBM per device.

v0:
```python
import jax
import jax.numpy as jnp
from jax import lax
from jax.sharding import Mesh
from jax.sharding import PartitionSpec as P

STATE = 128
BLOCK = 256
FEATURES = 2048
CTX = ("ctx_0", "ctx_1")
NORM_FLOOR = 0.25
HIGHEST = lax.Precision.HIGHEST


def from_behind(value, axis, steps):
    count = lax.axis_size(axis)
    first, last = (max(0, -steps), min(count, count - steps))
    return lax.ppermute(value, axis, [(source, source + steps) for source in range(first, last)])


def nothing_yet(x, identity):
    return jax.tree.map(
        lambda part, zero: jnp.zeros_like(part) + jnp.asarray(zero, part.dtype), x, identity
    )


def prefix_by_axis(x, axes, combine, identity):
    before = start = nothing_yet(x, identity)
    running = x
    for axis in reversed(axes):
        devices, mine = (lax.axis_size(axis), lax.axis_index(axis))
        pieces = jax.tree.map(
            lambda part, kind: lax.all_gather(part.astype(kind), axis),
            running,
            (jnp.bfloat16, jnp.bfloat16),
        )
        inside, running = (start, start)
        for k in range(devices):
            passed = k < mine
            running = combine(
                running, jax.tree.map(lambda part, own: part[k].astype(own.dtype), pieces, x)
            )
            inside = jax.tree.map(lambda new, old: jnp.where(passed, new, old), running, inside)
        before = combine(inside, before)
    return before


def gathered_total(x, axis):
    return lax.all_gather(x, axis).sum(0)


def sent_to_all(x, axis):
    copies = jnp.broadcast_to(x, (lax.axis_size(axis), *x.shape))
    return lax.all_to_all(copies, axis, split_axis=0, concat_axis=0, tiled=True)


def in_order(pieces, dim):
    pieces = jnp.moveaxis(pieces, 0, dim)
    lengths = pieces.shape
    return pieces.reshape(*lengths[:dim], lengths[dim] * lengths[dim + 1], *lengths[dim + 2 :])


def collect(x, axis, dim):
    pieces = sent_to_all(x, axis)
    return in_order(pieces, dim)


def shifted(value, axis, steps):
    count = lax.axis_size(axis)
    pairs = [(source, (source + steps) % count) for source in range(count)]
    return lax.ppermute(value, axis, pairs)


def causal_conv(sequence, previous, weights):
    length = sequence.shape[0]
    padded = jnp.concatenate([previous, sequence], axis=0).astype(jnp.float32)
    summed = jnp.zeros(sequence.shape, jnp.float32)
    for offset in range(weights.shape[0]):
        summed = summed + weights[offset] * padded[offset : offset + length]
    return summed


def chain_step(earlier, latter):
    return (earlier[0] + latter[0], jnp.exp(latter[0])[:, None, None] * earlier[1] + latter[1])


def shards(
    head_input,
    state_proj,
    gate_input,
    step_raw,
    step_bias,
    decay_log,
    skip_gain,
    conv_head,
    conv_state,
    norm_gain,
    next_weight,
):
    tap_count = conv_head.shape[1]
    token_count = head_input.shape[1]
    local_width = head_input.shape[2]
    head_count = step_raw.shape[1]
    head_width = local_width // head_count
    block_count = token_count // BLOCK
    tails = jnp.concatenate(
        [
            head_input[0, token_count - tap_count + 1 :],
            state_proj[0, token_count - tap_count + 1 :],
        ],
        axis=1,
    )
    previous = from_behind(tails, CTX, 1)
    conv_x = jax.nn.silu(
        causal_conv(head_input[0], previous[:, :local_width], conv_head[0])
    ).astype(jnp.bfloat16)
    conv_bc = causal_conv(state_proj[0], previous[:, local_width:], conv_state[0]).astype(
        jnp.bfloat16
    )
    blocks_x = conv_x.reshape(block_count, BLOCK, head_count, head_width)
    blocks_b = conv_bc[:, :STATE].reshape(block_count, BLOCK, STATE)
    blocks_c = conv_bc[:, STATE:].reshape(block_count, BLOCK, STATE)
    step_size = jax.nn.softplus(step_raw[0] + step_bias[0][:, None])
    log_decay = -jnp.exp(decay_log[0])[:, None] * step_size
    blocks_step = step_size.reshape(head_count, block_count, BLOCK)
    blocks_decay = log_decay.reshape(head_count, block_count, BLOCK)
    row_index = lax.broadcasted_iota(jnp.int32, (BLOCK, BLOCK), 0)
    col_index = lax.broadcasted_iota(jnp.int32, (BLOCK, BLOCK), 1)
    causal_mask = row_index >= col_index
    lower_tri = causal_mask.astype(jnp.float32)
    cumulative = jnp.einsum("hcs,ts->hct", blocks_decay, lower_tri, precision=HIGHEST)
    scores = jnp.einsum("ctn,csn->cts", blocks_c, blocks_b, preferred_element_type=jnp.float32)
    decay_diff = jnp.where(causal_mask, cumulative[..., :, None] - cumulative[..., None, :], 0.0)
    mix_weight = jnp.where(
        causal_mask, scores[None] * jnp.exp(decay_diff) * blocks_step[:, :, None, :], 0.0
    ).astype(jnp.bfloat16)
    intra_part = jnp.einsum(
        "hcts,cshp->cthp", mix_weight, blocks_x, preferred_element_type=jnp.float32
    )
    tail_weight = jnp.exp(cumulative[..., -1:] - cumulative) * blocks_step
    weighted_b = (blocks_b.astype(jnp.float32)[None] * tail_weight[..., None]).astype(jnp.bfloat16)
    updates = jnp.einsum(
        "cshp,hcsn->chpn", blocks_x, weighted_b, preferred_element_type=jnp.float32
    )
    totals = cumulative[..., -1]
    running = jnp.zeros((head_count, head_width, STATE), jnp.float32)
    before = jnp.zeros((head_count,), jnp.float32)
    entering = running
    offsets = before
    running = jnp.exp(totals[:, 0])[:, None, None] * running + updates[0]
    before = totals[:, 0]
    prior_log, prior_state = prefix_by_axis(
        (before, running), CTX, chain_step, (jnp.zeros_like(before), jnp.zeros_like(running))
    )
    full_states = jnp.stack([entering + jnp.exp(offsets)[:, None, None] * prior_state])
    inter_part = (
        jnp.einsum("ctn,chpn->cthp", blocks_c.astype(jnp.float32), full_states, precision=HIGHEST)
        * jnp.exp(cumulative).transpose(1, 2, 0)[..., None]
    )
    output = (
        intra_part + inter_part + skip_gain[0][None, None, :, None] * blocks_x.astype(jnp.float32)
    )
    gated = output.reshape(token_count, local_width) * jax.nn.silu(
        gate_input[0].astype(jnp.float32)
    )
    squares = gathered_total(jnp.sum(gated * gated, axis=1), "mp")
    mean_square = squares / FEATURES
    normed = (gated * lax.rsqrt(mean_square + NORM_FLOOR)[:, None] * norm_gain[0][None]).astype(
        jnp.bfloat16
    )
    gathered = collect(normed, "mp", 1)
    arrived = shifted(gathered, "section", 1)
    weight_rows = next_weight[0]
    full_weight = lax.all_gather(weight_rows, CTX, axis=0, tiled=True)
    result = jnp.dot(arrived, full_weight, preferred_element_type=jnp.float32)
    return result.astype(jnp.bfloat16)[None]


def solution(mesh):
    finer = Mesh(
        mesh.devices.reshape(mesh.shape["section"], 8, 8, mesh.shape["mp"]),
        ("section", "ctx_0", "ctx_1", "mp"),
    )
    in_specs = (
        P("section", CTX, "mp"),
        P("section", CTX, None),
        P("section", CTX, "mp"),
        P("section", "mp", CTX),
        P("section", "mp"),
        P("section", "mp"),
        P("section", "mp"),
        P("section", None, "mp"),
        P("section", None, None),
        P("section", "mp"),
        P("section", CTX, "mp"),
    )
    out_specs = P("section", CTX, "mp")
    return jax.shard_map(
        shards, mesh=finer, in_specs=in_specs, out_specs=out_specs, check_vma=False
    )
```

profile of v0, /device:TPU:1, one launch (start us, length us, event | category | flops | bytes accessed | tf_op | source)
XLA Modules:
  0.0 230.0 jit_solution(1536751369088576350)
XLA Ops:
  6.5 0.7 slice_bitcast_fusion.16
  7.3 0.7 slice_bitcast_fusion.17
  8.0 4.8 %collective-permute-start = (bf16[3,1280]{1,0:T(4,128)(2,1)S(1)}, bf16[3,1280]{1,0:T(4,128)(2,1)S(1)}, u32[]{:S(2)}, u32[]{:S(2)}) collective-permute-start(bf16[3,1280]{1,0:T(4,128)(2,1)S(1)} %pad_maximum_fusion), channel_id=1, source_target_pairs={{0,2},{2,4},{4,6},{6,8},{8,10},{10,12},{12,14},{14,16},{16,18},{18... | collective-permute-start | bytes 23048 | tf_op jit(solution)/shard_map/ppermute | solution.py:18
  12.8 0.7 negate_bitcast_fusion
  13.4 0.9 fusion.159
  14.3 0.8 compare_select_fusion
  15.3 0.3 multiply_reduce_fusion.1
  15.6 0.8 exponential_multiply_fusion
  16.4 0.8 fusion.160
  17.3 1.2 copy.20
  18.8 0.9 maximum_convert_fusion.1
  19.9 0.3 maximum_convert_fusion
  20.2 1.6 multiply_convert_fusion.2
  21.8 1.5 fusion.19
  23.5 1.3 dynamic-slice
  25.5 0.2 dynamic-update-slice
  25.7 17.4 %all-reduce = bf16[128]{0:T(256)(128)(2,1)S(1)} all-reduce(bf16[128]{0:T(256)(128)(2,1)S(1)} %dynamic-update-slice), channel_id=2, replica_groups=mesh['section'=4,'ctx_0'=8,'ctx_1'=8,'mp'=2] {'ctx_1'}, use_global_device_ids=true, to_apply=%add | all-reduce | flops 128 | bytes 512
  43.3 24.0 %all-gather.12.cloned.1.call-done = bf16[128,64,128]{2,1,0:T(8,128)(2,1)} async-done(((bf16[16,64,128]{2,1,0:T(8,128)(2,1)}), bf16[128,64,128]{2,1,0:T(8,128)(2,1)}) %all-gather.12.cloned.1.call-update) | async-done | bytes 2097168 | tf_op jit(solution)/shard_map/all_gather | solution.py:33
  67.4 2.8 %fusion.76 = bf16[1,16,64,128]{3,2,1,0:T(8,128)(2,1)} fusion(f32[16]{0:T(128)S(1)} %get-tuple-element.33, f32[16]{0:T(128)S(1)} %get-tuple-element.32, f32[16]{0:T(128)S(1)} %get-tuple-element.31, f32[16]{0:T(128)S(1)} %get-tuple-element.30, f32[16]{0:T(128)S(1)} %get-tuple-element.29, f32[16]{0:T(128)S(1)} %get-tuple-element.27, ...), kind=kLoop, calls=%fused_computation.93 | loop fusion | flops 3145728 | bytes 2359808 | tf_op jit(solution)/shard_map/convert_element_type | solution.py:33
  70.2 0.7 all-gather.14.cloned.1.call-update
  70.9 0.2 copy.22
  71.2 12.6 %all-gather.4 = bf16[8,1,16]{2,1,0:T(2,128)(2,1)S(1)} all-gather(bf16[1,1,16]{2,1,0:T(2,128)(2,1)S(1)} %convert_bitcast_fusion), channel_id=1, replica_groups=mesh['section'=4,'ctx_0'=8,'ctx_1'=8,'mp'=2] {'ctx_0'}, dimensions={0}, use_global_device_ids=true | all-gather | bytes 288 | tf_op jit(solution)/shard_map/all_gather | solution.py:33
  84.0 27.9 %all-gather.10.cloned.1.call-done = bf16[8,16,64,128]{3,2,1,0:T(8,128)(2,1)} async-done(((bf16[1,16,64,128]{3,2,1,0:T(8,128)(2,1)}), bf16[8,16,64,128]{3,2,1,0:T(8,128)(2,1)}) %all-gather.10.cloned.1.call-update) | async-done | bytes 2097168 | tf_op jit(solution)/shard_map/all_gather | solution.py:33
  111.9 3.6 %fusion.16 = f32[1,256,16,64]{1,3,2,0:T(8,128)S(1)} fusion(f32[256,16]{0,1:T(8,128)S(1)} %get-tuple-element.8, bf16[8,16,64,128]{3,2,1,0:T(8,128)(2,1)} %all-gather.10.cloned.1.call-done, f32[16]{0:T(128)S(1)} %get-tuple-element.33, f32[16]{0:T(128)S(1)} %get-tuple-element.32, f32[16]{0:T(128)S(1)} %get-tuple-element.31, f32[16]{0:T(128)S(1)} %get-tuple-element.30, ...), kind=kOutput, calls=%fused_computation.15 | convolution fusion | flops 411303936 | bytes 5333520 | tf_op jit(solution)/shard_map/ctn,chpn->cthp/dot_general | solution.py:157
  115.5 1.6 multiply_reduce_fusion
  117.2 6.3 %all-gather.5 = f32[2,1,256]{2,1,0:T(1,128)S(1)} all-gather(f32[1,1,256]{2,1,0:T(1,128)S(1)} %bitcast.274), channel_id=4, replica_groups=mesh['section'=4,'ctx_0'=8,'ctx_1'=8,'mp'=2] {'mp'}, dimensions={0}, use_global_device_ids=true | all-gather | bytes 3072 | tf_op jit(solution)/shard_map/all_gather | solution.py:49
  123.6 0.4 fusion.31
  124.0 4.5 %all_to_all.5 = bf16[2,256,1024]{1,2,0:T(8,128)(2,1)S(1)} all-to-all(bf16[2,256,1024]{1,2,0:T(8,128)(2,1)S(1)} %broadcast_in_dim.18), channel_id=1, replica_groups=mesh['section'=4,'ctx_0'=8,'ctx_1'=8,'mp'=2] {'mp'}, dimensions={0} | all-to-all | bytes 2097152 | tf_op jit(solution)/shard_map/all_to_all | solution.py:54
  128.6 3.1 %collective-permute-start.1 = (bf16[256,2048]{0,1:T(8,128)(2,1)S(1)}, bf16[256,2048]{0,1:T(8,128)(2,1)S(1)}, u32[]{:S(2)}, u32[]{:S(2)}) collective-permute-start(bf16[256,2048]{0,1:T(8,128)(2,1)S(1)} %bitcast.256), channel_id=1, source_target_pairs={{0,128},{128,256},{256,384},{384,0},{1,129},{129,257},{257,385},{3... | collective-permute-start | bytes 3145736 | tf_op jit(solution)/shard_map/ppermute | solution.py:71
  131.6 24.3 %collective-permute-done.1 = bf16[256,2048]{0,1:T(8,128)(2,1)S(1)} collective-permute-done((bf16[256,2048]{0,1:T(8,128)(2,1)S(1)}, bf16[256,2048]{0,1:T(8,128)(2,1)S(1)}, u32[]{:S(2)}, u32[]{:S(2)}) %collective-permute-start.1) | collective-permute-done | bytes 1048608 | tf_op jit(solution)/shard_map/ppermute | solution.py:71
  156.0 60.8 %all-gather.14.cloned.1.call-done = bf16[1,2048,2048]{2,1,0:T(8,128)(2,1)} async-done(((bf16[1,32,2048]{2,1,0:T(8,128)(2,1)}), bf16[1,2048,2048]{2,1,0:T(8,128)(2,1)}) %all-gather.14.cloned.1.call-update) | async-done | bytes 8388624 | tf_op jit(solution)/shard_map/all_gather | solution.py:174
  216.8 6.7 %fusion.5 = bf16[1,256,2048]{2,1,0:T(8,128)(2,1)} fusion(bf16[256,2048]{0,1:T(8,128)(2,1)S(1)} %collective-permute-done.1, bf16[1,2048,2048]{2,1,0:T(8,128)(2,1)} %all-gather.14.cloned.1.call-done), kind=kOutput, calls=%fused_computation.4 | convolution fusion | flops 2148007936 | bytes 10485760 | tf_op jit(solution)/shard_map/dot_general | solution.py:175
  (31 shorter events, 1.5 us)
Async XLA Ops:
  6.5 60.8 %all-gather.12.cloned.1.call-start = ((), (), s32[]{:S(2)}) async-start(), calls=%async_computation.2 | async-start | bytes 2359296 | tf_op jit(solution)/shard_map/all_gather | solution.py:33
  8.0 10.6 %collective-permute-start = (bf16[3,1280]{1,0:T(4,128)(2,1)S(1)}, bf16[3,1280]{1,0:T(4,128)(2,1)S(1)}, u32[]{:S(2)}, u32[]{:S(2)}) collective-permute-start(bf16[3,1280]{1,0:T(4,128)(2,1)S(1)} %pad_maximum_fusion), channel_id=1, source_target_pairs={{0,2},{2,4},{4,6},{6,8},{8,10},{10,12},{12,14},{14,16},{16,18},{18... | collective-permute-start | bytes 23048 | tf_op jit(solution)/shard_map/ppermute | solution.py:18
  21.8 49.1 %copy-start = (bf16[1,256,1024]{2,1,0:T(8,128)(2,1)S(1)}, bf16[1,256,1024]{2,1,0:T(8,128)(2,1)}, u32[]{:S(2)}) copy-start(bf16[1,256,1024]{2,1,0:T(8,128)(2,1)} %param.13) | copy-start | bytes 1572868
  23.4 88.5 %all-gather.10.cloned.1.call-start = ((), (), s32[]{:S(2)}) async-start(), calls=%async_computation.1 | async-start | bytes 2359296 | tf_op jit(solution)/shard_map/all_gather | solution.py:33
  70.2 146.6 %all-gather.14.cloned.1.call-start = ((), (), s32[]{:S(2)}) async-start(), calls=%async_computation.3 | async-start | bytes 8519680 | tf_op jit(solution)/shard_map/all_gather | solution.py:174
  111.9 3.6 %copy-start.2 = (f32[1,16]{1,0:T(1,128)S(1)}, f32[1,16]{1,0:T(1,128)}, u32[]{:S(2)}) copy-start(f32[1,16]{1,0:T(1,128)} %param.17) | copy-start | bytes 196
  115.5 8.0 %copy-start.1 = (f32[1,1024]{1,0:T(1,128)S(1)}, f32[1,1024]{1,0:T(1,128)}, u32[]{:S(2)}) copy-start(f32[1,1024]{1,0:T(1,128)} %param.20) | copy-start | bytes 12292
  128.6 27.4 %collective-permute-start.1 = (bf16[256,2048]{0,1:T(8,128)(2,1)S(1)}, bf16[256,2048]{0,1:T(8,128)(2,1)S(1)}, u32[]{:S(2)}, u32[]{:S(2)}) collective-permute-start(bf16[256,2048]{0,1:T(8,128)(2,1)S(1)} %bitcast.256), channel_id=1, source_target_pairs={{0,128},{128,256},{256,384},{384,0},{1,129},{129,257},{257,385},{3... | collective-permute-start | bytes 3145736 | tf_op jit(solution)/shard_map/ppermute | solution.py:71
Sparse Core Ops, SparseCore 0:
  23.5 43.8 all-gather.11
  70.3 41.5 all-gather.9
  114.9 101.8 all-gather.13
where the time goes:
time: 231 us; the launch traced here: 230 us
  waiting for transfers between devices  138 us (60%)
  blocking collectives  40.8 us (18%)
  between operations  13.9 us (6%)
  matrix products  13.8 us (6%)
  other arithmetic  9.13 us (4%)
  starting transfers between devices  7.98 us (3%)
  local copies, waits for them, and re-layouts  6.58 us (3%)
    all_gather x1, waiting for transfers between devices, shards(): full_weight = lax.all_gather(weight_rows, CTX, axis=0, tiled=True)  60.8 us
    all_gather x2, waiting for transfers between devices, prefix_by_axis(): lax.all_gather(part.astype(kind), axis)  51.9 us
    ppermute x1, waiting for transfers between devices, shifted(): return lax.ppermute(value, axis, pairs)  24.3 us
    unnamed x1, blocking collectives  17.4 us
    all_gather x1, blocking collectives, prefix_by_axis(): lax.all_gather(part.astype(kind), axis)  12.6 us
    dot_general x1, matrix products, shards(): result = jnp.dot(arrived, full_weight, preferred_element_type=jnp.float32)  6.7 us
    all_gather x1, blocking collectives, gathered_total(): return lax.all_gather(x, axis).sum(0)  6.34 us
    ppermute x1, starting transfers between devices, from_behind(): lax.ppermute(value, axis, [(source, source + steps) for source in range(f...  4.81 us
  transfers between devices with their start and end apart: 5, of which 4 were waited for; matrix products, arithmetic and copies ran while one was open for 6% of the time, Pallas kernels for 0%

commit v1 on v0

--- a/solution.py
+++ b/solution.py
@@ -171,7 +171,9 @@
     gathered = collect(normed, "mp", 1)
     arrived = shifted(gathered, "section", 1)
     weight_rows = next_weight[0]
-    full_weight = lax.all_gather(weight_rows, CTX, axis=0, tiled=True)
+    full_weight = jnp.concatenate(
+        lax.all_to_all(jnp.stack([weight_rows] * lax.axis_size(CTX)), CTX, 0, 0), axis=0
+    )
     result = jnp.dot(arrived, full_weight, preferred_element_type=jnp.float32)
     return result.astype(jnp.bfloat16)[None]
 

time: 231 us -> 437 us (1.89)
  the two profiles are of different devices: /device:TPU:1 before, /device:TPU:136 now
where the time goes in v1:
time: 437 us; the launch traced here: 436 us
  waiting for transfers between devices  331 us (76%)
  blocking collectives  38.5 us (9%)
  starting transfers between devices  18.5 us (4%)
  between operations  14.2 us (3%)
  matrix products  13.8 us (3%)
  local copies, waits for them, and re-layouts  10.9 us (2%)
  other arithmetic  9.12 us (2%)
    all_to_all x1, waiting for transfers between devices, shards(): lax.all_to_all(jnp.stack([weight_rows] * lax.axis_size(CTX)), CTX, 0, 0)  254 us
    all_gather x2, waiting for transfers between devices, prefix_by_axis(): lax.all_gather(part.astype(kind), axis)  52.6 us
    ppermute x1, waiting for transfers between devices, shifted(): return lax.ppermute(value, axis, pairs)  24.4 us
    unnamed x1, blocking collectives  17.1 us
    all_gather x1, blocking collectives, prefix_by_axis(): lax.all_gather(part.astype(kind), axis)  15 us
    all_to_all x1, starting transfers between devices, shards(): lax.all_to_all(jnp.stack([weight_rows] * lax.axis_size(CTX)), CTX, 0, 0)  10.8 us
  transfers between devices with their start and end apart: 5, of which 4 were waited for; matrix products, arithmetic and copies ran while one was open for 2% of the time, Pallas kernels for 0%

profile of v1, /device:TPU:136, one launch (start us, length us, event | category | flops | bytes accessed | tf_op | source)
XLA Modules:
  0.0 436.5 jit_solution(8976270813851337264)
XLA Ops:
  6.5 0.7 slice_bitcast_fusion.17
  7.2 0.7 slice_bitcast_fusion.16
  8.0 4.3 collective-permute-start
  12.3 0.7 negate_bitcast_fusion
  12.9 0.8 compare_select_fusion
  13.9 0.3 multiply_reduce_fusion.1
  14.2 0.9 fusion.152
  15.1 0.8 exponential_multiply_fusion
  15.9 0.8 fusion.153
  16.8 1.2 copy.20
  18.2 0.9 maximum_convert_fusion.1
  19.3 0.3 maximum_convert_fusion
  19.7 1.6 multiply_convert_fusion.2
  21.3 1.5 fusion.12
  22.9 1.3 dynamic-slice
  24.9 0.2 dynamic-update-slice
  25.2 17.1 %all-reduce = bf16[128]{0:T(256)(128)(2,1)S(1)} all-reduce(bf16[128]{0:T(256)(128)(2,1)S(1)} %dynamic-update-slice), channel_id=2, replica_groups=mesh['section'=4,'ctx_0'=8,'ctx_1'=8,'mp'=2] {'ctx_1'}, use_global_device_ids=true, to_apply=%add | all-reduce | flops 128 | bytes 512
  42.5 25.3 %all-gather.10.cloned.1.call-done = bf16[128,64,128]{2,1,0:T(8,128)(2,1)} async-done(((bf16[16,64,128]{2,1,0:T(8,128)(2,1)}), bf16[128,64,128]{2,1,0:T(8,128)(2,1)}) %all-gather.10.cloned.1.call-update) | async-done | bytes 2097168 | tf_op jit(solution)/shard_map/all_gather | solution.py:33
  67.8 2.8 fusion.69
  70.9 15.0 %all-gather.3 = bf16[8,1,16]{2,1,0:T(2,128)(2,1)S(1)} all-gather(bf16[1,1,16]{2,1,0:T(2,128)(2,1)S(1)} %convert_bitcast_fusion), channel_id=1, replica_groups=mesh['section'=4,'ctx_0'=8,'ctx_1'=8,'mp'=2] {'ctx_0'}, dimensions={0}, use_global_device_ids=true | all-gather | bytes 288 | tf_op jit(solution)/shard_map/all_gather | solution.py:33
  86.2 27.3 %all-gather.8.cloned.1.call-done = bf16[8,16,64,128]{3,2,1,0:T(8,128)(2,1)} async-done(((bf16[1,16,64,128]{3,2,1,0:T(8,128)(2,1)}), bf16[8,16,64,128]{3,2,1,0:T(8,128)(2,1)}) %all-gather.8.cloned.1.call-update) | async-done | bytes 2097168 | tf_op jit(solution)/shard_map/all_gather | solution.py:33
  113.5 3.6 fusion.9
  117.1 1.6 multiply_reduce_fusion
  118.8 1.8 all-gather.4
  120.6 0.4 fusion.24
  121.1 4.6 %all_to_all.10 = bf16[2,256,1024]{1,2,0:T(8,128)(2,1)S(1)} all-to-all(bf16[2,256,1024]{1,2,0:T(8,128)(2,1)S(1)} %broadcast_in_dim.18), channel_id=1, replica_groups=mesh['section'=4,'ctx_0'=8,'ctx_1'=8,'mp'=2] {'mp'}, dimensions={0} | all-to-all | bytes 2097152 | tf_op jit(solution)/shard_map/all_to_all | solution.py:54
  125.7 4.3 stack.4
  129.9 10.8 %all-to-all-start.1 = ((bf16[64,32,2048]{2,1,0:T(8,128)(2,1)}), bf16[64,32,2048]{2,1,0:T(8,128)(2,1)}, u32[]{:S(2)}, u32[]{:S(2)}) async-start(bf16[64,32,2048]{2,1,0:T(8,128)(2,1)} %stack.4), calls=%async_computation.1 | async-start | bytes 16777216 | tf_op jit(solution)/shard_map/all_to_all | solution.py:175
  140.7 3.4 collective-permute-start.1
  144.1 24.4 %collective-permute-done.1 = bf16[256,2048]{0,1:T(8,128)(2,1)S(1)} collective-permute-done((bf16[256,2048]{0,1:T(8,128)(2,1)S(1)}, bf16[256,2048]{0,1:T(8,128)(2,1)S(1)}, u32[]{:S(2)}, u32[]{:S(2)}) %collective-permute-start.1) | collective-permute-done | bytes 1048608 | tf_op jit(solution)/shard_map/ppermute | solution.py:71
  168.5 254.4 %all-to-all-done.1 = bf16[64,32,2048]{2,1,0:T(8,128)(2,1)} async-done(((bf16[64,32,2048]{2,1,0:T(8,128)(2,1)}), bf16[64,32,2048]{2,1,0:T(8,128)(2,1)}, u32[]{:S(2)}, u32[]{:S(2)}) %all-to-all-start.1) | async-done | bytes 8388640 | tf_op jit(solution)/shard_map/all_to_all | solution.py:175
  422.9 6.7 %fusion = bf16[1,256,2048]{2,1,0:T(8,128)(2,1)} fusion(bf16[256,2048]{0,1:T(8,128)(2,1)S(1)} %collective-permute-done.1, bf16[2048,2048]{1,0:T(8,128)(2,1)} %bitcast.73), kind=kOutput, calls=%fused_computation.2 | convolution fusion | flops 2148007936 | bytes 10485760 | tf_op jit(solution)/shard_map/dot_general | solution.py:177
  (33 shorter events, 1.7 us)
Async XLA Ops:
  6.5 61.3 %all-gather.10.cloned.1.call-start = ((), (), s32[]{:S(2)}) async-start(), calls=%async_computation.3 | async-start | bytes 2359296 | tf_op jit(solution)/shard_map/all_gather | solution.py:33
  8.0 10.0 %collective-permute-start = (bf16[3,1280]{1,0:T(4,128)(2,1)S(1)}, bf16[3,1280]{1,0:T(4,128)(2,1)S(1)}, u32[]{:S(2)}, u32[]{:S(2)}) collective-permute-start(bf16[3,1280]{1,0:T(4,128)(2,1)S(1)} %pad_maximum_fusion), channel_id=1, source_target_pairs={{0,2},{2,4},{4,6},{6,8},{8,10},{10,12},{12,14},{14,16},{16,18},{18... | collective-permute-start | bytes 23048 | tf_op jit(solution)/shard_map/ppermute | solution.py:18
  21.3 49.4 %copy-start = (bf16[1,256,1024]{2,1,0:T(8,128)(2,1)S(1)}, bf16[1,256,1024]{2,1,0:T(8,128)(2,1)}, u32[]{:S(2)}) copy-start(bf16[1,256,1024]{2,1,0:T(8,128)(2,1)} %param.13) | copy-start | bytes 1572868
  22.8 90.7 %all-gather.8.cloned.1.call-start = ((), (), s32[]{:S(2)}) async-start(), calls=%async_computation.2 | async-start | bytes 2359296 | tf_op jit(solution)/shard_map/all_gather | solution.py:33
  113.5 3.6 copy-start.3
  117.1 3.5 copy-start.2
  121.0 4.7 %copy-start.1 = (bf16[1,32,2048]{2,1,0:T(8,128)(2,1)S(1)}, bf16[1,32,2048]{2,1,0:T(8,128)(2,1)}, u32[]{:S(2)}) copy-start(bf16[1,32,2048]{2,1,0:T(8,128)(2,1)} %param.21) | copy-start | bytes 393220
  129.9 293.0 %all-to-all-start.1 = ((bf16[64,32,2048]{2,1,0:T(8,128)(2,1)}), bf16[64,32,2048]{2,1,0:T(8,128)(2,1)}, u32[]{:S(2)}, u32[]{:S(2)}) async-start(bf16[64,32,2048]{2,1,0:T(8,128)(2,1)} %stack.4), calls=%async_computation.1 | async-start | bytes 16777216 | tf_op jit(solution)/shard_map/all_to_all | solution.py:175
  140.7 27.7 %collective-permute-start.1 = (bf16[256,2048]{0,1:T(8,128)(2,1)S(1)}, bf16[256,2048]{0,1:T(8,128)(2,1)S(1)}, u32[]{:S(2)}, u32[]{:S(2)}) collective-permute-start(bf16[256,2048]{0,1:T(8,128)(2,1)S(1)} %bitcast.252), channel_id=1, source_target_pairs={{0,128},{128,256},{256,384},{384,0},{1,129},{129,257},{257,385},{3... | collective-permute-start | bytes 3145736 | tf_op jit(solution)/shard_map/ppermute | solution.py:71
Sparse Core Ops, SparseCore 0:
  23.0 44.8 all-gather.9
  70.7 42.7 all-gather.7
